TPU v7x, 32 devices: a whole 2x2x4 slice. The times are simulated.
32 devices in a mesh: gx: 4 (over z), gy: 2 (over y), gz: 4 (over x, core).
Axes of the slice: x: 2, y: 2, z: 4, core: 2. Of those that a mesh axis runs over, the one named last changes fastest.
Arguments:
- coords: float32 [3, 65536], P(None, ('gx', 'gy', 'gz')), may hold values from 0 to 3
- anchor: float32 [3, 65536], P(None, ('gx', 'gy', 'gz')), may hold values from -73 to 76
- atom_types: int32 [65536], P(('gx', 'gy', 'gz')), may hold values from 0 to 63
- halo_send: int32 [27904], P(('gx', 'gy', 'gz')), may hold values from 0 to 2047, as said below
- neighbours: int32 [8192, 8], P(('gx', 'gy', 'gz')), may hold values from 0 to 364, as said below
- live_counts: int32 [8192], P(('gx', 'gy', 'gz')), may hold values from 1 to 8
- rep_coef: float32 [64], replicated, may hold values from 0.5 to 2
- disp_coef: float32 [64], replicated, may hold values from 0.2 to 1
- charge: float32 [64], replicated, may hold values from -1 to 1
- step_history: float32 [8, 3, 65536], P(None, None, ('gx', 'gy', 'gz')), may hold values from -9 to 9
- grad_history: float32 [8, 3, 65536], P(None, None, ('gx', 'gy', 'gz')), may hold values from -72 to 72, as said below
Outputs:
- new_coords: float32 [3, 65536], P(None, ('gx', 'gy', 'gz'))
- energy: float32 [], replicated
Inputs may be any that keep to these rules, and one draw needn't show every extreme that they name: `halo_send`: each of a domain's seven blocks holds distinct local atom indices, rising. `neighbours`: slot 0 of row r is r mod 256, the row's own cluster. `grad_history`: the product of each entry with the matching step_history entry is not negative, and each pair's inner product is positive.
All inputs are finite; a program needn't handle non-finite values.
Results may differ from a plain program's by a relative error of at most 0.0003.
Values sent between devices are 32-bit elements; how exact they have to be, the bound alone decides.
No kernel may reach another device: no remote copies, remote signals or barrier semaphores. Data moves between devices by JAX's collectives and lax.ppermute only.
A program may use at most 64 MiB of HBM per device.

v0:
```python
import math
import jax
import jax.numpy as jnp
from jax import lax
from jax.sharding import PartitionSpec as P

domain_side = 3.0
step_length = 0.5
axis_bits = {"gx": 4, "gy": 2, "gz": 1}
axis_component = {"gx": 0, "gy": 1, "gz": 2}


def shifted(value, axis, steps):
    count = lax.axis_size(axis)
    pairs = [(source, (source + steps) % count) for source in range(count)]
    return lax.ppermute(value, axis, pairs)


def export_sizes(atoms_local):
    face_rows = atoms_local // 8
    edge_rows = max(atoms_local // 64, 8)
    corner_rows = max(atoms_local // 512, 8)
    return [face_rows, face_rows, edge_rows, face_rows, edge_rows, edge_rows, corner_rows]


def tile_gradient(ext_pos, ext_par, neighbours, live_counts):
    highest = lax.Precision.HIGHEST
    ext_clusters = ext_pos.shape[1] // 8
    pos_tiles = ext_pos.reshape(3, ext_clusters, 8).transpose(0, 2, 1)
    par_tiles = ext_par.reshape(3, ext_clusters, 8).transpose(0, 2, 1)
    both_tiles = jnp.concatenate([pos_tiles, par_tiles], axis=0)
    cluster_rows = neighbours.shape[0]
    list_width = neighbours.shape[1]
    block_rows = math.gcd(256, cluster_rows)
    block_count = cluster_rows // block_rows
    atom_rank = jnp.arange(8, dtype=jnp.int32)
    ordered_pair = (atom_rank[:, None] < atom_rank[None, :]).astype(jnp.float32)[:, :, None]
    slot_rank = jnp.tile(jnp.arange(list_width, dtype=jnp.int32), block_rows)
    ext_ids = jnp.arange(ext_clusters, dtype=jnp.int32)

    def one_block(state_pair, block_id):
        gradient, energy = state_pair
        first_row = block_id * block_rows
        listed = neighbours.reshape(-1)
        selector = (listed[:, None] == ext_ids[None, :]).astype(jnp.float32)
        live_count = jnp.repeat(live_counts, list_width)
        home_ids = jnp.repeat(first_row + jnp.arange(block_rows, dtype=jnp.int32), list_width)
        live_mask = (slot_rank < live_count).astype(jnp.float32)
        weight = live_mask[None, None, :] * jnp.where(
            (listed == home_ids)[None, None, :], ordered_pair, 1.0
        )
        pos_home = jnp.repeat(
            lax.dynamic_slice_in_dim(pos_tiles, first_row, block_rows, 2), list_width, axis=2
        )
        par_home = jnp.repeat(
            lax.dynamic_slice_in_dim(par_tiles, first_row, block_rows, 2), list_width, axis=2
        )
        other_tiles = jnp.einsum("caj,kj->cak", both_tiles, selector, precision=highest)
        pos_other = other_tiles[:3]
        par_other = other_tiles[3:]
        offset = pos_home[:, :, None, :] - pos_other[:, None, :, :]
        dist_sq = jnp.sum(offset * offset, axis=0)
        inverse = 1.0 / (1.0 + dist_sq)
        repulse = par_home[0][:, None, :] * par_other[0][None, :, :]
        attract = par_home[1][:, None, :] * par_other[1][None, :, :]
        coulomb = par_home[2][:, None, :] * par_other[2][None, :, :]
        root_inv = jnp.sqrt(inverse)
        pair_energy = repulse * inverse * inverse - attract * inverse + coulomb * root_inv
        slope = 2.0 * repulse * inverse - attract + 0.5 * coulomb / root_inv
        factor = -2.0 * weight * slope * inverse * inverse
        push_term = factor[None] * offset
        home_grad = jnp.sum(push_term, axis=2).reshape(3, 8, block_rows, list_width).sum(axis=3)
        other_grad = -jnp.sum(push_term, axis=1)
        gradient = gradient + jnp.einsum("cak,kj->caj", other_grad, selector, precision=highest)
        current = lax.dynamic_slice_in_dim(gradient, first_row, block_rows, 2)
        gradient = lax.dynamic_update_slice_in_dim(gradient, current + home_grad, first_row, 2)
        energy = energy + jnp.sum(weight * pair_energy)
        return ((gradient, energy), None)

    initial = (jnp.zeros((3, 8, ext_clusters), jnp.float32), jnp.zeros((), jnp.float32))
    (gradient, energy), unused = lax.scan(
        one_block, initial, jnp.arange(block_count, dtype=jnp.int32)
    )
    return (gradient.transpose(0, 2, 1).reshape(3, -1), energy)


def pass_along(payload, axis_name, offset):
    if axis_name == "gx":
        return shifted(payload, "gx", offset)
    if axis_name == "gy":
        return shifted(payload, "gy", offset)
    return shifted(payload, "gz", offset)


def two_loop(cross_products, grad_dots):
    memory = cross_products.shape[0] // 2
    basis_size = 2 * memory + 1
    gram_full = jnp.zeros((basis_size, basis_size), jnp.float32)
    gram_full = (
        gram_full.at[0, 1:].set(grad_dots).at[1:, 0].set(grad_dots).at[1:, 1:].set(cross_products)
    )
    unit_rows = jnp.eye(basis_size, dtype=jnp.float32)
    inverse_sy = [1.0 / cross_products[hist_id, memory + hist_id] for hist_id in range(memory)]
    alphas = [None] * memory
    coeffs = unit_rows[0]
    for hist_id in reversed(range(memory)):
        alphas[hist_id] = inverse_sy[hist_id] * jnp.sum(gram_full[1 + hist_id] * coeffs)
        coeffs = coeffs - alphas[hist_id] * unit_rows[1 + memory + hist_id]
    scaling = (
        cross_products[memory - 1, 2 * memory - 1] / cross_products[2 * memory - 1, 2 * memory - 1]
    )
    coeffs = scaling * coeffs
    for hist_id in range(memory):
        beta_term = inverse_sy[hist_id] * jnp.sum(gram_full[1 + memory + hist_id] * coeffs)
        coeffs = coeffs + (alphas[hist_id] - beta_term) * unit_rows[1 + hist_id]
    return coeffs


def on_device(
    coords,
    anchor,
    atom_types,
    halo_send,
    neighbours,
    live_counts,
    rep_coef,
    disp_coef,
    charge,
    step_history,
    grad_history,
):
    highest = lax.Precision.HIGHEST
    atoms_local = coords.shape[1]
    size_list = export_sizes(atoms_local)
    start_list = [sum(size_list[:block_pos]) for block_pos in range(7)]
    history = jnp.concatenate([step_history, grad_history], axis=0).reshape(
        2 * step_history.shape[0], -1
    )
    type_table = jnp.stack([rep_coef, disp_coef, charge])
    type_ids = jnp.arange(type_table.shape[1], dtype=jnp.int32)
    one_hot = (atom_types[None, :] == type_ids[:, None]).astype(jnp.float32)
    params = jnp.dot(type_table, one_hot, precision=highest)
    local_rows = jnp.concatenate([coords, params], axis=0)
    exported = jnp.take(local_rows, halo_send, axis=1)
    axis_order = ["gz", "gy", "gx"]
    held_blocks = {}
    for block_code in range(1, 8):
        block_start = start_list[block_code - 1]
        held_blocks[block_code] = exported[:, block_start : block_start + size_list[block_code - 1]]
    for axis_name in axis_order:
        bit_value = axis_bits[axis_name]
        movers = [block_code for block_code in range(1, 8) if block_code & bit_value]
        payload = jnp.concatenate([held_blocks[block_code] for block_code in movers], axis=1)
        arrived = pass_along(payload, axis_name, -1)
        moved_by = jnp.array(
            [
                domain_side if component == axis_component[axis_name] else 0.0
                for component in range(6)
            ],
            jnp.float32,
        )
        arrived = arrived + moved_by[:, None]
        cursor = 0
        for block_code in movers:
            held_blocks[block_code] = arrived[:, cursor : cursor + size_list[block_code - 1]]
            cursor = cursor + size_list[block_code - 1]
    halo_part = jnp.concatenate([held_blocks[block_code] for block_code in range(1, 8)], axis=1)
    extended = jnp.concatenate([local_rows, halo_part], axis=1)
    gradient_ext, energy_local = tile_gradient(extended[:3], extended[3:], neighbours, live_counts)
    gradient = gradient_ext[:, :atoms_local]
    back_blocks = {}
    for block_code in range(1, 8):
        begin = atoms_local + start_list[block_code - 1]
        back_blocks[block_code] = gradient_ext[:, begin : begin + size_list[block_code - 1]]
    for axis_name in reversed(axis_order):
        bit_value = axis_bits[axis_name]
        movers = [block_code for block_code in range(1, 8) if block_code & bit_value]
        payload = jnp.concatenate([back_blocks[block_code] for block_code in movers], axis=1)
        arrived = pass_along(payload, axis_name, 1)
        cursor = 0
        for block_code in movers:
            back_blocks[block_code] = arrived[:, cursor : cursor + size_list[block_code - 1]]
            cursor = cursor + size_list[block_code - 1]
    returned = jnp.concatenate([back_blocks[block_code] for block_code in range(1, 8)], axis=1)
    gradient = gradient.at[:, halo_send].add(returned)
    displacement = coords - anchor
    gradient = gradient + displacement
    energy_local = energy_local + 0.5 * jnp.sum(displacement * displacement)
    flat_grad = gradient.reshape(-1)
    grad_dots_local = jnp.dot(history, flat_grad, precision=highest)
    cross_products, grad_dots, energy_sum = lax.psum(
        (jnp.dot(history, history.T, precision=highest), grad_dots_local, energy_local),
        ("gx", "gy", "gz"),
    )
    coeffs = two_loop(cross_products, grad_dots)
    basis_rows = jnp.concatenate([flat_grad[None], history], axis=0)
    direction = jnp.dot(coeffs, basis_rows, precision=highest).reshape(3, atoms_local)
    new_coords = coords - step_length * direction
    atoms_total = atoms_local * lax.axis_size("gx") * lax.axis_size("gy") * lax.axis_size("gz")
    return (new_coords, energy_sum / atoms_total)


def solution(mesh):
    placed = (
        P(None, ("gx", "gy", "gz")),
        P(None, ("gx", "gy", "gz")),
        P(("gx", "gy", "gz")),
        P(("gx", "gy", "gz")),
        P(("gx", "gy", "gz"), None),
        P(("gx", "gy", "gz")),
        P(),
        P(),
        P(),
        P(None, None, ("gx", "gy", "gz")),
        P(None, None, ("gx", "gy", "gz")),
    )
    return jax.shard_map(
        on_device,
        mesh=mesh,
        in_specs=placed,
        out_specs=(P(None, ("gx", "gy", "gz")), P()),
        check_vma=False,
    )
```

profile of v0, /device:TPU:12, one launch (start us, length us, event | category | flops | bytes accessed | tf_op | source)
XLA Modules:
  0.0 138.7 jit_solution(14454354531783564797)
XLA Ops:
  0.7 0.7 compare_select_fusion
  1.4 0.7 compare_and_fusion
  2.1 1.0 fusion.20
  3.1 0.8 pad_maximum_fusion
  3.9 0.4 copy.62
  4.3 1.9 %gather_fusion = f32[872,6]{1,0:T(8,128)S(1)} fusion(f32[6,2048]{0,1:T(8,128)S(1)} %copy.62, s32[1024]{0:T(1024)S(1)} %pad_clamp_fusion), kind=kCustom, calls=%fused_computation | custom fusion | bytes 45344 | tf_op jit(solution)/shard_map/jit(_take)/gather | solution.py:144
  6.7 0.9 collective-permute-start
  7.8 1.2 collective-permute-done
  9.4 0.5 collective-permute-start.1
  9.9 1.2 convolution_bitcast_fusion
  11.1 1.9 %collective-permute-done.1 = f32[6,328]{1,0:T(8,128)S(1)} collective-permute-done((f32[6,328]{1,0:T(8,128)S(1)}, f32[6,328]{1,0:T(8,128)S(1)}, u32[]{:S(2)}, u32[]{:S(2)}) %collective-permute-start.1) | collective-permute-done | bytes 7904 | tf_op jit(solution)/shard_map/ppermute | solution.py:16
  13.3 0.5 collective-permute-start.2
  14.2 0.6 eq.79
  14.8 2.2 %collective-permute-done.2 = f32[6,328]{1,0:T(8,128)S(1)} collective-permute-done((f32[6,328]{1,0:T(8,128)S(1)}, f32[6,328]{1,0:T(8,128)S(1)}, u32[]{:S(2)}, u32[]{:S(2)}) %collective-permute-start.2) | collective-permute-done | bytes 7904 | tf_op jit(solution)/shard_map/ppermute | solution.py:16
  18.3 1.2 fusion.3
  19.5 0.7 slice.459
  20.2 0.7 slice_bitcast_fusion.7
  20.8 0.8 slice_bitcast_fusion.1
  21.6 0.7 copy.67
  22.3 1.6 %broadcast_in_dim.99 = f32[3,8,256,8]{3,2,1,0:T(8,128)S(1)} broadcast(f32[3,8,256]{2,1,0:T(8,128)} %copy.67), dimensions={0,1,2} | broadcast | bytes 221184 | tf_op jit(solution)/shard_map/while/body/eval_jaxpr/broadcast_in_dim | solution.py:52
  24.0 2.8 %sub.111 = f32[3,8,2048]{2,1,0:T(8,128)} reshape(f32[3,8,256,8]{3,2,1,0:T(8,128)S(1)} %broadcast_in_dim.99) | data formatting | bytes 393216 | tf_op jit(solution)/shard_map/while/body/eval_jaxpr/sub | solution.py:61
  26.7 1.1 slice_bitcast_fusion.4
  28.2 0.5 broadcast_in_dim.101
  29.1 0.5 broadcast_in_dim.103
  30.1 0.5 broadcast_in_dim.98
  30.8 1.0 fusion.18
  31.8 1.3 fusion.5
  33.1 2.7 %reshape.266 = f32[3,8,256,8]{3,2,1,0:T(8,128)S(1)} reshape(f32[3,8,2048]{2,1,0:T(8,128)} %get-tuple-element.71) | data formatting | bytes 393216 | tf_op jit(solution)/shard_map/while/body/eval_jaxpr/reshape | solution.py:72
  35.8 3.0 %fusion.1 = f32[3,8,365]{2,1,0:T(8,128)} fusion(s32[2048]{0:T(1024)S(1)} %copy-done.10, f32[3,8,2048]{2,1,0:T(8,128)} %get-tuple-element.72), kind=kOutput, calls=%fused_computation.4 | convolution fusion | flops 216082432 | bytes 239840 | tf_op jit(solution)/shard_map/while/body/eval_jaxpr/cak,kj->caj/dot_general | solution.py:74
  38.8 1.5 %reduce_sum.206 = f32[3,8,256]{2,1,0:T(8,128)} reduce(f32[3,8,256,8]{3,2,1,0:T(8,128)S(1)} %reshape.266, f32[]{:T(128)} %constant.140.clone.1), dimensions={3}, to_apply=%region_4.5 | reduce | flops 43008 | bytes 221188 | tf_op jit(solution)/shard_map/while/body/eval_jaxpr/reduce_sum | solution.py:72
  40.3 1.4 fusion.28
  41.6 1.0 copy.70
  43.0 1.8 %collective-permute-start.3 = (f32[3,328]{1,0:T(4,128)S(1)}, f32[3,328]{1,0:T(4,128)S(1)}, u32[]{:S(2)}, u32[]{:S(2)}) collective-permute-start(f32[3,328]{1,0:T(4,128)S(1)} %slice.467), channel_id=1, source_target_pairs={{0,8},{8,16},{16,24},{24,0},{1,9},{9,17},{17,25},{25,1},{2,10},{10... | collective-permute-start | bytes 11816 | tf_op jit(solution)/shard_map/ppermute | solution.py:16
  44.7 2.0 %collective-permute-done.3 = f32[3,328]{1,0:T(4,128)S(1)} collective-permute-done((f32[3,328]{1,0:T(4,128)S(1)}, f32[3,328]{1,0:T(4,128)S(1)}, u32[]{:S(2)}, u32[]{:S(2)}) %collective-permute-start.3) | collective-permute-done | bytes 3968 | tf_op jit(solution)/shard_map/ppermute | solution.py:16
  46.9 0.5 collective-permute-start.4
  47.4 0.7 fusion.90
  48.2 2.4 %collective-permute-done.4 = f32[3,328]{1,0:T(4,128)S(1)} collective-permute-done((f32[3,328]{1,0:T(4,128)S(1)}, f32[3,328]{1,0:T(4,128)S(1)}, u32[]{:S(2)}, u32[]{:S(2)}) %collective-permute-start.4) | collective-permute-done | bytes 3968 | tf_op jit(solution)/shard_map/ppermute | solution.py:16
  50.8 0.6 multiply_reduce_fusion
  51.4 0.4 copy.71
  53.1 0.7 collective-permute-done.5
  54.3 6.4 %scatter_fusion = f32[3,2048]{0,1:T(8,128)S(1)} fusion(f32[3,2048]{0,1:T(8,128)S(1)} %copy.71, s32[872]{0:T(1024)S(1)} %compare_select_fusion, f32[872,3]{1,0:T(8,128)S(1)} %copy.72), kind=kCustom, calls=%fused_computation.1 | custom fusion | flops 2616 | bytes 34880 | tf_op jit(solution)/shard_map/scatter-add | solution.py:185
  61.4 0.6 convolution_bitcast_fusion.1
  62.0 42.8 %all-reduce = (f32[16,16]{1,0:T(8,128)S(1)}, f32[16]{0:T(128)S(1)}, f32[]{:T(128)}) all-reduce(f32[16,16]{1,0:T(8,128)S(1)} %copy-done.8, f32[16]{0:T(128)S(1)} %convolution_bitcast_fusion.1, f32[]{:T(128)S(6)} %add.171), channel_id=1, replica_groups=mesh['gx'=4,'gy'=2,'gz'=4] {'gx','gy','gz'}, use_global_device_ids=true, to_apply=%region_0.1 | all-reduce | flops 273 | bytes 2184 | tf_op jit(solution)/shard_map/psum | solution.py:191
  104.8 0.7 fusion.87
  105.5 1.6 %scatter.10 = f32[17,17]{1,0:T(8,128)S(1)} dynamic-update-slice(f32[17,17]{1,0:T(8,128)S(1)} %broadcast_in_dim.88, f32[1,16]{1,0:T(1,128)S(1)} %bitcast.102, s32[]{:T(128)} %bitcast.23, s32[]{:T(128)} %bitcast.24) | dynamic-update-slice | bytes 132 | tf_op jit(solution)/shard_map/scatter | solution.py:100
  107.4 0.8 scatter.14
  110.1 0.6 fusion.68
  111.3 0.7 fusion.66
  114.0 0.6 fusion.64
  115.3 0.7 fusion.62
  117.9 0.6 fusion.60
  119.1 0.7 fusion.58
  121.8 0.6 fusion.56
  122.9 0.7 fusion.54
  125.0 0.7 fusion.52
  126.3 0.6 fusion.50
  127.5 0.7 fusion.48
  128.8 0.7 fusion.46
  130.1 0.7 fusion.44
  131.4 0.6 fusion.42
  132.7 0.6 fusion.40
  133.9 0.6 fusion.38
  135.6 0.6 fusion.10
  136.2 0.6 fusion.27
  (104 shorter events, 7.0 us)
Async XLA Ops:
  0.6 7.0 %copy-start.6 = (f32[8,3,2048]{2,0,1:T(8,128)S(1)}, f32[8,3,2048]{2,0,1:T(8,128)}, u32[]{:S(2)}) copy-start(f32[8,3,2048]{2,0,1:T(8,128)} %param.29) | copy-start | bytes 589828
  0.6 7.0 %copy-start.7 = (f32[8,3,2048]{2,0,1:T(8,128)S(1)}, f32[8,3,2048]{2,0,1:T(8,128)}, u32[]{:S(2)}) copy-start(f32[8,3,2048]{2,0,1:T(8,128)} %param.30) | copy-start | bytes 589828
  0.7 7.1 %copy-start.14 = (s32[256]{0:T(256)S(1)}, s32[256]{0:T(256)}, u32[]{:S(2)}) copy-start(s32[256]{0:T(256)} %param.25) | copy-start | bytes 3076
  3.1 6.0 %copy-start.17 = (f32[6]{0:T(128)S(1)}, f32[6]{0:T(128)}, u32[]{:S(2)}) copy-start(f32[6]{0:T(128)} %constant.151.clone) | copy-start | bytes 76
  4.3 8.8 %copy-start.16 = (f32[6]{0:T(128)S(1)}, f32[6]{0:T(128)}, u32[]{:S(2)}) copy-start(f32[6]{0:T(128)} %constant.152.clone) | copy-start | bytes 76
  4.3 9.5 %copy-start.13 = (s32[256,8]{0,1:T(8,128)S(1)}, s32[256,8]{0,1:T(8,128)}, u32[]{:S(2)}) copy-start(s32[256,8]{0,1:T(8,128)} %param.24) | copy-start | bytes 24580
  6.2 10.8 %copy-start.15 = (f32[6]{0:T(128)S(1)}, f32[6]{0:T(128)}, u32[]{:S(2)}) copy-start(f32[6]{0:T(128)} %constant.153.clone) | copy-start | bytes 76
  6.7 2.3 %collective-permute-start = (f32[6,328]{1,0:T(8,128)S(1)}, f32[6,328]{1,0:T(8,128)S(1)}, u32[]{:S(2)}, u32[]{:S(2)}) collective-permute-start(f32[6,328]{1,0:T(8,128)S(1)} %pad_maximum_fusion.1), channel_id=1, source_target_pairs={{0,3},{1,0},{2,1},{3,2},{4,7},{5,4},{6,5},{7,6},{8,11},{9,8},{10,9... | collective-permute-start | bytes 23624 | tf_op jit(solution)/shard_map/ppermute | solution.py:16
  9.4 3.7 %collective-permute-start.1 = (f32[6,328]{1,0:T(8,128)S(1)}, f32[6,328]{1,0:T(8,128)S(1)}, u32[]{:S(2)}, u32[]{:S(2)}) collective-permute-start(f32[6,328]{1,0:T(8,128)S(1)} %pad_maximum_fusion.2), channel_id=1, source_target_pairs={{0,4},{4,0},{1,5},{5,1},{2,6},{6,2},{3,7},{7,3},{8,12},{12,8},{9,1... | collective-permute-start | bytes 23624 | tf_op jit(solution)/shard_map/ppermute | solution.py:16
  13.3 3.7 %collective-permute-start.2 = (f32[6,328]{1,0:T(8,128)S(1)}, f32[6,328]{1,0:T(8,128)S(1)}, u32[]{:S(2)}, u32[]{:S(2)}) collective-permute-start(f32[6,328]{1,0:T(8,128)S(1)} %pad_maximum_fusion.3), channel_id=1, source_target_pairs={{0,24},{8,0},{16,8},{24,16},{1,25},{9,1},{17,9},{25,17},{2,26},{10... | collective-permute-start | bytes 23624 | tf_op jit(solution)/shard_map/ppermute | solution.py:16
  14.0 4.3 %copy-start.9 = (s32[2048]{0:T(1024)}, s32[2048]{0:T(1024)S(1)}, u32[]{:S(2)}) copy-start(s32[2048]{0:T(1024)S(1)} %reshape.262) | copy-start | bytes 24580
  29.1 1.5 %copy-start = (f32[3,8,2048]{2,1,0:T(8,128)S(1)}, f32[3,8,2048]{2,1,0:T(8,128)}, u32[]{:S(2)}) copy-start(f32[3,8,2048]{2,1,0:T(8,128)} %slice.459) | copy-start | bytes 589828
  29.1 1.5 %copy-start.1 = (f32[3,8,2048]{2,1,0:T(8,128)S(1)}, f32[3,8,2048]{2,1,0:T(8,128)}, u32[]{:S(2)}) copy-start(f32[3,8,2048]{2,1,0:T(8,128)} %sub.111) | copy-start | bytes 589828
  29.7 1.1 copy-start.3
  29.7 1.1 copy-start.4
  29.7 1.1 copy-start.5
  29.7 1.1 copy-start.12
  33.1 2.7 %copy-start.10 = (s32[2048]{0:T(1024)S(1)}, s32[2048]{0:T(1024)}, u32[]{:S(2)}) copy-start(s32[2048]{0:T(1024)} %copy-done.9) | copy-start | bytes 24580
  40.2 10.5 %copy-start.2 = (f32[3,2048]{1,0:T(4,128)S(1)}, f32[3,2048]{1,0:T(4,128)}, u32[]{:S(2)}) copy-start(f32[3,2048]{1,0:T(4,128)} %param.20) | copy-start | bytes 73732
  40.2 10.6 %copy-start.11 = (f32[3,2048]{1,0:T(4,128)S(1)}, f32[3,2048]{1,0:T(4,128)}, u32[]{:S(2)}) copy-start(f32[3,2048]{1,0:T(4,128)} %param.21) | copy-start | bytes 73732
  43.0 3.8 %collective-permute-start.3 = (f32[3,328]{1,0:T(4,128)S(1)}, f32[3,328]{1,0:T(4,128)S(1)}, u32[]{:S(2)}, u32[]{:S(2)}) collective-permute-start(f32[3,328]{1,0:T(4,128)S(1)} %slice.467), channel_id=1, source_target_pairs={{0,8},{8,16},{16,24},{24,0},{1,9},{9,17},{17,25},{25,1},{2,10},{10... | collective-permute-start | bytes 11816 | tf_op jit(solution)/shard_map/ppermute | solution.py:16
  46.9 3.6 %collective-permute-start.4 = (f32[3,328]{1,0:T(4,128)S(1)}, f32[3,328]{1,0:T(4,128)S(1)}, u32[]{:S(2)}, u32[]{:S(2)}) collective-permute-start(f32[3,328]{1,0:T(4,128)S(1)} %pad_maximum_fusion.4), channel_id=1, source_target_pairs={{0,4},{4,0},{1,5},{5,1},{2,6},{6,2},{3,7},{7,3},{8,12},{12,8},{9,1... | collective-permute-start | bytes 11816 | tf_op jit(solution)/shard_map/ppermute | solution.py:16
  50.8 3.1 %collective-permute-start.5 = (f32[3,328]{1,0:T(4,128)S(1)}, f32[3,328]{1,0:T(4,128)S(1)}, u32[]{:S(2)}, u32[]{:S(2)}) collective-permute-start(f32[3,328]{1,0:T(4,128)S(1)} %pad_maximum_fusion.5), channel_id=1, source_target_pairs={{0,1},{1,2},{2,3},{3,0},{4,5},{5,6},{6,7},{7,4},{8,9},{9,10},{10,1... | collective-permute-start | bytes 11816 | tf_op jit(solution)/shard_map/ppermute | solution.py:16
  54.1 7.9 %copy-start.8 = (f32[16,16]{1,0:T(8,128)S(1)}, f32[16,16]{1,0:T(8,128)}, u32[]{:S(2)}) copy-start(f32[16,16]{1,0:T(8,128)} %convolution_bitcast_fusion) | copy-start | bytes 3076
where the time goes:
time: 140 us; the launch traced here: 139 us
  blocking collectives  42.8 us (31%)
  other arithmetic  26.8 us (19%)
  local copies, waits for them, and re-layouts  25.8 us (18%)
  between operations  20.9 us (15%)
  waiting for transfers between devices  10.5 us (8%)
  matrix products  7.65 us (5%)
  starting transfers between devices  4.16 us (3%)
    psum x1, blocking collectives, on_device(): lax.psum((jnp.dot(history, history.T, precision=highest), grad_dots_local...  42.8 us
    ppermute x6, waiting for transfers between devices, shifted(): return lax.ppermute(value, axis, pairs)  10.5 us
    scatter-add x1, other arithmetic, on_device(): gradient = gradient.at[:, halo_send].add(returned)  6.44 us
    reduce_sum x8, other arithmetic, two_loop(): jnp.sum(gram_full[1 + memory + hist_id] * coeffs)  5.12 us
    reduce_sum x8, other arithmetic, two_loop(): jnp.sum(gram_full[1 + hist_id] * coeffs)  5.11 us
    ppermute x6, starting transfers between devices, shifted(): return lax.ppermute(value, axis, pairs)  4.16 us
    dot_general x1, matrix products, one_block(): jnp.einsum('cak,kj->caj', other_grad, selector, precision=highest)  2.95 us
  transfers between devices with their start and end apart: 6, of which 6 were waited for; matrix products, arithmetic and copies ran while one was open for 3% of the time, Pallas kernels for 0%

commit v1 on v0

--- a/solution.py
+++ b/solution.py
@@ -189,8 +189,11 @@
     flat_grad = gradient.reshape(-1)
     grad_dots_local = jnp.dot(history, flat_grad, precision=highest)
     cross_products, grad_dots, energy_sum = lax.psum(
-        (jnp.dot(history, history.T, precision=highest), grad_dots_local, energy_local),
-        ("gx", "gy", "gz"),
+        lax.psum(
+            (jnp.dot(history, history.T, precision=highest), grad_dots_local, energy_local),
+            ("gy", "gz"),
+        ),
+        "gx",
     )
     coeffs = two_loop(cross_products, grad_dots)
     basis_rows = jnp.concatenate([flat_grad[None], history], axis=0)

time: 140 us -> 128 us (0.914)
  the two profiles are of different devices: /device:TPU:12 before, /device:TPU:0 now
where the time goes in v1:
time: 128 us; the launch traced here: 127 us
  other arithmetic  26.8 us (21%)
  blocking collectives  26.1 us (20%)
  local copies, waits for them, and re-layouts  25.8 us (20%)
  between operations  20.9 us (16%)
  waiting for transfers between devices  10 us (8%)
  starting transfers between devices  9.5 us (7%)
  matrix products  7.65 us (6%)
    psum x1, blocking collectives, on_device(): lax.psum((jnp.dot(history, history.T, precision=highest), grad_dots_local...  14.8 us
    psum x1, blocking collectives, on_device(): lax.psum(lax.psum((jnp.dot(history, history.T, precision=highest), grad_d...  11.3 us
    ppermute x6, waiting for transfers between devices, shifted(): return lax.ppermute(value, axis, pairs)  10 us
    ppermute x6, starting transfers between devices, shifted(): return lax.ppermute(value, axis, pairs)  9.5 us
    scatter-add x1, other arithmetic, on_device(): gradient = gradient.at[:, halo_send].add(returned)  6.44 us
    reduce_sum x8, other arithmetic, two_loop(): jnp.sum(gram_full[1 + memory + hist_id] * coeffs)  5.12 us
    reduce_sum x8, other arithmetic, two_loop(): jnp.sum(gram_full[1 + hist_id] * coeffs)  5.11 us
    dot_general x1, matrix products, one_block(): jnp.einsum('cak,kj->caj', other_grad, selector, precision=highest)  2.95 us
  transfers between devices with their start and end apart: 6, of which 6 were waited for; matrix products, arithmetic and copies ran while one was open for 3% of the time, Pallas kernels for 0%

profile of v1, /device:TPU:0, one launch (start us, length us, event | category | flops | bytes accessed | tf_op | source)
XLA Modules:
  0.0 126.8 jit_solution(4249474000943316165)
XLA Ops:
  0.7 0.7 compare_select_fusion
  1.4 0.7 compare_and_fusion
  2.1 1.0 fusion.20
  3.1 0.8 pad_maximum_fusion
  3.9 0.4 copy.62
  4.3 1.9 %gather_fusion = f32[872,6]{1,0:T(8,128)S(1)} fusion(f32[6,2048]{0,1:T(8,128)S(1)} %copy.62, s32[1024]{0:T(1024)S(1)} %pad_clamp_fusion), kind=kCustom, calls=%fused_computation | custom fusion | bytes 45344 | tf_op jit(solution)/shard_map/jit(_take)/gather | solution.py:144
  6.7 2.4 %collective-permute-start = (f32[6,328]{1,0:T(8,128)S(1)}, f32[6,328]{1,0:T(8,128)S(1)}, u32[]{:S(2)}, u32[]{:S(2)}) collective-permute-start(f32[6,328]{1,0:T(8,128)S(1)} %pad_maximum_fusion.1), channel_id=1, source_target_pairs={{0,3},{1,0},{2,1},{3,2},{4,7},{5,4},{6,5},{7,6},{8,11},{9,8},{10,9... | collective-permute-start | bytes 23624 | tf_op jit(solution)/shard_map/ppermute | solution.py:16
  9.3 1.2 collective-permute-done
  10.8 1.5 %collective-permute-start.1 = (f32[6,328]{1,0:T(8,128)S(1)}, f32[6,328]{1,0:T(8,128)S(1)}, u32[]{:S(2)}, u32[]{:S(2)}) collective-permute-start(f32[6,328]{1,0:T(8,128)S(1)} %pad_maximum_fusion.2), channel_id=1, source_target_pairs={{0,4},{4,0},{1,5},{5,1},{2,6},{6,2},{3,7},{7,3},{8,12},{12,8},{9,1... | collective-permute-start | bytes 23624 | tf_op jit(solution)/shard_map/ppermute | solution.py:16
  12.4 1.2 convolution_bitcast_fusion
  13.6 0.9 collective-permute-done.1
  14.8 3.6 %collective-permute-start.2 = (f32[6,328]{1,0:T(8,128)S(1)}, f32[6,328]{1,0:T(8,128)S(1)}, u32[]{:S(2)}, u32[]{:S(2)}) collective-permute-start(f32[6,328]{1,0:T(8,128)S(1)} %pad_maximum_fusion.3), channel_id=1, source_target_pairs={{0,24},{8,0},{16,8},{24,16},{1,25},{9,1},{17,9},{25,17},{2,26},{10... | collective-permute-start | bytes 23624 | tf_op jit(solution)/shard_map/ppermute | solution.py:16
  18.9 0.6 eq.79
  21.1 1.2 fusion.3
  22.3 0.7 slice.459
  23.0 0.7 slice_bitcast_fusion.7
  23.6 0.8 slice_bitcast_fusion.1
  24.4 0.7 copy.67
  25.1 1.6 %broadcast_in_dim.99 = f32[3,8,256,8]{3,2,1,0:T(8,128)S(1)} broadcast(f32[3,8,256]{2,1,0:T(8,128)} %copy.67), dimensions={0,1,2} | broadcast | bytes 221184 | tf_op jit(solution)/shard_map/while/body/eval_jaxpr/broadcast_in_dim | solution.py:52
  26.7 2.8 %sub.111 = f32[3,8,2048]{2,1,0:T(8,128)} reshape(f32[3,8,256,8]{3,2,1,0:T(8,128)S(1)} %broadcast_in_dim.99) | data formatting | bytes 393216 | tf_op jit(solution)/shard_map/while/body/eval_jaxpr/sub | solution.py:61
  29.5 1.1 slice_bitcast_fusion.4
  31.0 0.5 broadcast_in_dim.101
  31.9 0.5 broadcast_in_dim.103
  32.9 0.5 broadcast_in_dim.98
  33.6 1.0 fusion.18
  34.6 1.3 fusion.5
  35.9 2.7 %reshape.266 = f32[3,8,256,8]{3,2,1,0:T(8,128)S(1)} reshape(f32[3,8,2048]{2,1,0:T(8,128)} %get-tuple-element.71) | data formatting | bytes 393216 | tf_op jit(solution)/shard_map/while/body/eval_jaxpr/reshape | solution.py:72
  38.6 3.0 %fusion.1 = f32[3,8,365]{2,1,0:T(8,128)} fusion(s32[2048]{0:T(1024)S(1)} %copy-done.10, f32[3,8,2048]{2,1,0:T(8,128)} %get-tuple-element.72), kind=kOutput, calls=%fused_computation.4 | convolution fusion | flops 216082432 | bytes 239840 | tf_op jit(solution)/shard_map/while/body/eval_jaxpr/cak,kj->caj/dot_general | solution.py:74
  41.5 1.5 %reduce_sum.206 = f32[3,8,256]{2,1,0:T(8,128)} reduce(f32[3,8,256,8]{3,2,1,0:T(8,128)S(1)} %reshape.266, f32[]{:T(128)} %constant.140.clone.1), dimensions={3}, to_apply=%region_5.6 | reduce | flops 43008 | bytes 221188 | tf_op jit(solution)/shard_map/while/body/eval_jaxpr/reduce_sum | solution.py:72
  43.0 1.4 %fusion.28 = f32[3,8,365]{2,1,0:T(8,128)} fusion(f32[3,8,365]{2,1,0:T(8,128)} %fusion.1, f32[3,8,256]{2,1,0:T(8,128)} %reduce_sum.206), kind=kLoop, calls=%fused_computation.59 | loop fusion | flops 6144 | bytes 73728 | tf_op jit(solution)/shard_map/while/body/eval_jaxpr/dynamic_update_slice | solution.py:76
  44.4 1.0 copy.70
  45.8 0.4 collective-permute-start.3
  46.2 5.4 %collective-permute-done.3 = f32[3,328]{1,0:T(4,128)S(1)} collective-permute-done((f32[3,328]{1,0:T(4,128)S(1)}, f32[3,328]{1,0:T(4,128)S(1)}, u32[]{:S(2)}, u32[]{:S(2)}) %collective-permute-start.3) | collective-permute-done | bytes 3968 | tf_op jit(solution)/shard_map/ppermute | solution.py:16
  51.8 1.5 %collective-permute-start.4 = (f32[3,328]{1,0:T(4,128)S(1)}, f32[3,328]{1,0:T(4,128)S(1)}, u32[]{:S(2)}, u32[]{:S(2)}) collective-permute-start(f32[3,328]{1,0:T(4,128)S(1)} %pad_maximum_fusion.4), channel_id=1, source_target_pairs={{0,4},{4,0},{1,5},{5,1},{2,6},{6,2},{3,7},{7,3},{8,12},{12,8},{9,1... | collective-permute-start | bytes 11816 | tf_op jit(solution)/shard_map/ppermute | solution.py:16
  53.3 0.7 fusion.90
  54.0 1.4 %collective-permute-done.4 = f32[3,328]{1,0:T(4,128)S(1)} collective-permute-done((f32[3,328]{1,0:T(4,128)S(1)}, f32[3,328]{1,0:T(4,128)S(1)}, u32[]{:S(2)}, u32[]{:S(2)}) %collective-permute-start.4) | collective-permute-done | bytes 3968 | tf_op jit(solution)/shard_map/ppermute | solution.py:16
  55.7 0.6 multiply_reduce_fusion
  56.3 0.4 copy.71
  58.0 0.7 collective-permute-done.5
  59.2 6.4 %scatter_fusion = f32[3,2048]{0,1:T(8,128)S(1)} fusion(f32[3,2048]{0,1:T(8,128)S(1)} %copy.71, s32[872]{0:T(1024)S(1)} %compare_select_fusion, f32[872,3]{1,0:T(8,128)S(1)} %copy.72), kind=kCustom, calls=%fused_computation.1 | custom fusion | flops 2616 | bytes 34880 | tf_op jit(solution)/shard_map/scatter-add | solution.py:185
  66.3 0.6 convolution_bitcast_fusion.1
  66.9 14.8 %all-reduce = (f32[16,16]{1,0:T(8,128)S(1)}, f32[16]{0:T(128)S(1)}, f32[]{:T(128)}) all-reduce(f32[16,16]{1,0:T(8,128)S(1)} %copy-done.8, f32[16]{0:T(128)S(1)} %convolution_bitcast_fusion.1, f32[]{:T(128)S(6)} %add.177), channel_id=1, replica_groups=mesh['gx'=4,'gy'=2,'gz'=4] {'gy','gz'}, use_global_device_ids=true, to_apply=%region_0.1 | all-reduce | flops 273 | bytes 2184 | tf_op jit(solution)/shard_map/psum | solution.py:192
  81.6 11.3 %all-reduce.1 = (f32[16,16]{1,0:T(8,128)S(1)}, f32[16]{0:T(128)S(1)}, f32[]{:T(128)}) all-reduce(f32[16,16]{1,0:T(8,128)S(1)} %get-tuple-element.73, f32[16]{0:T(128)S(1)} %get-tuple-element.74, f32[]{:T(128)} %get-tuple-element.75), channel_id=1, replica_groups=mesh['gx'=4,'gy'=2,'gz'=4] {'gx'}, use_global_device_ids=true, to_apply=%region_1.2 | all-reduce | flops 273 | bytes 2184 | tf_op jit(solution)/shard_map/psum | solution.py:191
  92.9 0.7 fusion.87
  93.7 1.6 %scatter.10 = f32[17,17]{1,0:T(8,128)S(1)} dynamic-update-slice(f32[17,17]{1,0:T(8,128)S(1)} %broadcast_in_dim.88, f32[1,16]{1,0:T(1,128)S(1)} %bitcast.102, s32[]{:T(128)} %bitcast.23, s32[]{:T(128)} %bitcast.24) | dynamic-update-slice | bytes 132 | tf_op jit(solution)/shard_map/scatter | solution.py:100
  95.6 0.8 scatter.14
  98.2 0.6 fusion.68
  99.5 0.7 fusion.66
  102.2 0.6 fusion.64
  103.4 0.7 fusion.62
  106.1 0.6 fusion.60
  107.2 0.7 fusion.58
  109.9 0.6 fusion.56
  111.1 0.7 fusion.54
  113.1 0.7 fusion.52
  114.4 0.6 fusion.50
  115.6 0.7 fusion.48
  116.9 0.7 fusion.46
  118.2 0.7 fusion.44
  119.5 0.6 fusion.42
  120.8 0.6 fusion.40
  122.1 0.6 fusion.38
  123.7 0.6 fusion.10
  124.4 0.6 fusion.27
  (105 shorter events, 7.3 us)
Async XLA Ops:
  0.6 8.5 %copy-start.6 = (f32[8,3,2048]{2,0,1:T(8,128)S(1)}, f32[8,3,2048]{2,0,1:T(8,128)}, u32[]{:S(2)}) copy-start(f32[8,3,2048]{2,0,1:T(8,128)} %param.29) | copy-start | bytes 589828
  0.6 8.5 %copy-start.7 = (f32[8,3,2048]{2,0,1:T(8,128)S(1)}, f32[8,3,2048]{2,0,1:T(8,128)}, u32[]{:S(2)}) copy-start(f32[8,3,2048]{2,0,1:T(8,128)} %param.30) | copy-start | bytes 589828
  0.7 8.5 %copy-start.14 = (s32[256]{0:T(256)S(1)}, s32[256]{0:T(256)}, u32[]{:S(2)}) copy-start(s32[256]{0:T(256)} %param.25) | copy-start | bytes 3076
  3.1 7.4 %copy-start.17 = (f32[6]{0:T(128)S(1)}, f32[6]{0:T(128)}, u32[]{:S(2)}) copy-start(f32[6]{0:T(128)} %constant.151.clone) | copy-start | bytes 76
  4.3 10.3 %copy-start.16 = (f32[6]{0:T(128)S(1)}, f32[6]{0:T(128)}, u32[]{:S(2)}) copy-start(f32[6]{0:T(128)} %constant.152.clone) | copy-start | bytes 76
  4.3 14.1 %copy-start.13 = (s32[256,8]{0,1:T(8,128)S(1)}, s32[256,8]{0,1:T(8,128)}, u32[]{:S(2)}) copy-start(s32[256,8]{0,1:T(8,128)} %param.24) | copy-start | bytes 24580
  6.2 13.6 %copy-start.15 = (f32[6]{0:T(128)S(1)}, f32[6]{0:T(128)}, u32[]{:S(2)}) copy-start(f32[6]{0:T(128)} %constant.153.clone) | copy-start | bytes 76
  6.7 3.8 %collective-permute-start = (f32[6,328]{1,0:T(8,128)S(1)}, f32[6,328]{1,0:T(8,128)S(1)}, u32[]{:S(2)}, u32[]{:S(2)}) collective-permute-start(f32[6,328]{1,0:T(8,128)S(1)} %pad_maximum_fusion.1), channel_id=1, source_target_pairs={{0,3},{1,0},{2,1},{3,2},{4,7},{5,4},{6,5},{7,6},{8,11},{9,8},{10,9... | collective-permute-start | bytes 23624 | tf_op jit(solution)/shard_map/ppermute | solution.py:16
  10.8 3.7 %collective-permute-start.1 = (f32[6,328]{1,0:T(8,128)S(1)}, f32[6,328]{1,0:T(8,128)S(1)}, u32[]{:S(2)}, u32[]{:S(2)}) collective-permute-start(f32[6,328]{1,0:T(8,128)S(1)} %pad_maximum_fusion.2), channel_id=1, source_target_pairs={{0,4},{4,0},{1,5},{5,1},{2,6},{6,2},{3,7},{7,3},{8,12},{12,8},{9,1... | collective-permute-start | bytes 23624 | tf_op jit(solution)/shard_map/ppermute | solution.py:16
  14.8 5.0 %collective-permute-start.2 = (f32[6,328]{1,0:T(8,128)S(1)}, f32[6,328]{1,0:T(8,128)S(1)}, u32[]{:S(2)}, u32[]{:S(2)}) collective-permute-start(f32[6,328]{1,0:T(8,128)S(1)} %pad_maximum_fusion.3), channel_id=1, source_target_pairs={{0,24},{8,0},{16,8},{24,16},{1,25},{9,1},{17,9},{25,17},{2,26},{10... | collective-permute-start | bytes 23624 | tf_op jit(solution)/shard_map/ppermute | solution.py:16
  18.6 2.4 %copy-start.9 = (s32[2048]{0:T(1024)}, s32[2048]{0:T(1024)S(1)}, u32[]{:S(2)}) copy-start(s32[2048]{0:T(1024)S(1)} %reshape.262) | copy-start | bytes 24580
  31.9 1.5 %copy-start = (f32[3,8,2048]{2,1,0:T(8,128)S(1)}, f32[3,8,2048]{2,1,0:T(8,128)}, u32[]{:S(2)}) copy-start(f32[3,8,2048]{2,1,0:T(8,128)} %slice.459) | copy-start | bytes 589828
  31.9 1.5 %copy-start.1 = (f32[3,8,2048]{2,1,0:T(8,128)S(1)}, f32[3,8,2048]{2,1,0:T(8,128)}, u32[]{:S(2)}) copy-start(f32[3,8,2048]{2,1,0:T(8,128)} %sub.111) | copy-start | bytes 589828
  32.5 1.1 copy-start.3
  32.5 1.1 copy-start.4
  32.5 1.1 copy-start.5
  32.5 1.1 copy-start.12
  35.9 2.7 %copy-start.10 = (s32[2048]{0:T(1024)S(1)}, s32[2048]{0:T(1024)}, u32[]{:S(2)}) copy-start(s32[2048]{0:T(1024)} %copy-done.9) | copy-start | bytes 24580
  43.0 12.6 %copy-start.2 = (f32[3,2048]{1,0:T(4,128)S(1)}, f32[3,2048]{1,0:T(4,128)}, u32[]{:S(2)}) copy-start(f32[3,2048]{1,0:T(4,128)} %param.20) | copy-start | bytes 73732
  43.0 12.6 %copy-start.11 = (f32[3,2048]{1,0:T(4,128)S(1)}, f32[3,2048]{1,0:T(4,128)}, u32[]{:S(2)}) copy-start(f32[3,2048]{1,0:T(4,128)} %param.21) | copy-start | bytes 73732
  45.8 5.9 %collective-permute-start.3 = (f32[3,328]{1,0:T(4,128)S(1)}, f32[3,328]{1,0:T(4,128)S(1)}, u32[]{:S(2)}, u32[]{:S(2)}) collective-permute-start(f32[3,328]{1,0:T(4,128)S(1)} %slice.467), channel_id=1, source_target_pairs={{0,8},{8,16},{16,24},{24,0},{1,9},{9,17},{17,25},{25,1},{2,10},{10... | collective-permute-start | bytes 11816 | tf_op jit(solution)/shard_map/ppermute | solution.py:16
  51.8 3.6 %collective-permute-start.4 = (f32[3,328]{1,0:T(4,128)S(1)}, f32[3,328]{1,0:T(4,128)S(1)}, u32[]{:S(2)}, u32[]{:S(2)}) collective-permute-start(f32[3,328]{1,0:T(4,128)S(1)} %pad_maximum_fusion.4), channel_id=1, source_target_pairs={{0,4},{4,0},{1,5},{5,1},{2,6},{6,2},{3,7},{7,3},{8,12},{12,8},{9,1... | collective-permute-start | bytes 11816 | tf_op jit(solution)/shard_map/ppermute | solution.py:16
  55.6 3.1 %collective-permute-start.5 = (f32[3,328]{1,0:T(4,128)S(1)}, f32[3,328]{1,0:T(4,128)S(1)}, u32[]{:S(2)}, u32[]{:S(2)}) collective-permute-start(f32[3,328]{1,0:T(4,128)S(1)} %pad_maximum_fusion.5), channel_id=1, source_target_pairs={{0,1},{1,2},{2,3},{3,0},{4,5},{5,6},{6,7},{7,4},{8,9},{9,10},{10,1... | collective-permute-start | bytes 11816 | tf_op jit(solution)/shard_map/ppermute | solution.py:16
  58.9 7.9 %copy-start.8 = (f32[16,16]{1,0:T(8,128)S(1)}, f32[16,16]{1,0:T(8,128)}, u32[]{:S(2)}) copy-start(f32[16,16]{1,0:T(8,128)} %convolution_bitcast_fusion) | copy-start | bytes 3076
